TPU v7x, 32 devices: a whole 2x2x4 slice. The times are simulated.
32 devices in a mesh: groups: 2 (over y), ctx: 4 (over z), head: 2 (over x), rep: 2 (over core).
Axes of the slice: x: 2, y: 2, z: 4, core: 2. Of those that a mesh axis runs over, the one named last changes fastest.
Arguments:
- queries: bfloat16 [2048, 4096], P(('groups', 'ctx'), ('head', 'rep')), parts along dimension 0, may hold values from -24 to 24
- keys: bfloat16 [2048, 1024], P(('groups', 'ctx'), ('head', 'rep')), parts along dimension 0, may hold values from -6 to 6
- values: bfloat16 [2048, 1024], P(('groups', 'ctx'), ('head', 'rep')), parts along dimension 0, may hold values from -6 to 6
- span_order: int32 [8], replicated, may hold values from 0 to 7, as said below
Outputs:
- attended: bfloat16 [2048, 4096], P(('groups', 'ctx'), ('head', 'rep')), parts along dimension 0
There are 2 independent parts, one for each index of `groups`. A program takes and returns all parts, laid end to end along the dimension named above; an argument that names none is the same for every part. Nothing has to cross between parts.
Inputs may be any that keep to these rules, and one draw needn't show every extreme that they name: `span_order`: A permutation of the spans in which entries 2 d and 2 d + 1 are c and 7 - c for some c.
All inputs are finite; a program needn't handle non-finite values.
Results may differ from a plain program's by a relative error of at most 0.0047.
Values may be sent and summed in bfloat16 or wider, within the bound.
A program may use at most 64 MiB of HBM per device.

v0:
```python
import math
import jax
import jax.numpy as jnp
from jax import lax
from jax.sharding import PartitionSpec as P

HEAD_SIZE = 128
masked_score = -1e30


def lookup_positions(span_order, first_row, row_count, span_rows):
    row_ids = first_row + jnp.arange(row_count, dtype=jnp.int32)
    span_ids = row_ids // span_rows
    span_table = jnp.arange(span_order.shape[0], dtype=jnp.int32)
    span_starts = jnp.sum(
        jnp.where(span_ids[:, None] == span_table[None, :], span_order[None, :], 0), axis=1
    )
    return span_starts * span_rows + row_ids % span_rows


def source_partials(query_block, query_pos, key_group, value_group, key_pos, head_dim):
    score_scale = 1.0 / math.sqrt(head_dim)
    scores = (
        jnp.einsum("rhgd,cshd->crhgs", query_block, key_group, preferred_element_type=jnp.float32)
        * score_scale
    )
    allowed = (key_pos[:, None, :] <= query_pos[None, :, None])[:, :, None, None, :]
    masked = jnp.where(allowed, scores, masked_score)
    row_top = jnp.max(masked, axis=-1)
    weights = jnp.where(allowed, jnp.exp(masked - row_top[..., None]), 0.0)
    row_total = jnp.sum(weights, axis=-1)
    numerator = jnp.einsum(
        "crhgs,cshd->crhgd",
        weights.astype(jnp.bfloat16),
        value_group,
        preferred_element_type=jnp.float32,
    )
    partial_value = (numerator / jnp.maximum(row_total, 1.0)[..., None]).astype(jnp.bfloat16)
    return (partial_value, row_top, row_total)


def absorb(running, partial_value, row_top, row_total):
    run_top, run_total, run_sum = running
    new_top = jnp.maximum(run_top, row_top)
    rescale = jnp.exp(run_top - new_top)
    source_weight = row_total * jnp.exp(row_top - new_top)
    return (
        new_top,
        run_total * rescale + source_weight,
        run_sum * rescale[..., None] + source_weight[..., None] * partial_value.astype(jnp.float32),
    )


def shards(queries, keys, values, span_order):
    rows_here = queries.shape[0]
    span_rows = rows_here // 2
    head_dim = HEAD_SIZE
    kv_heads = keys.shape[1] // head_dim
    common_values = queries.shape[1] // keys.shape[1]
    my_index = lax.axis_index("ctx")
    own_pos = lookup_positions(span_order, my_index * rows_here, rows_here, span_rows)
    q_local = queries.reshape(rows_here, kv_heads, common_values, head_dim)
    initial = (
        jnp.full((rows_here, kv_heads, common_values), masked_score, jnp.float32),
        jnp.zeros((rows_here, kv_heads, common_values), jnp.float32),
        jnp.zeros((rows_here, kv_heads, common_values, head_dim), jnp.float32),
    )
    running = initial
    k_piece = lax.all_gather(keys, "ctx", axis=0, tiled=True)
    v_piece = lax.all_gather(values, "ctx", axis=0, tiled=True)
    shard_count = k_piece.shape[0] // rows_here
    per_turn = 2
    turn_count = shard_count // per_turn
    k_pos = lookup_positions(span_order, jnp.int32(0), k_piece.shape[0], span_rows)
    k_steps = k_piece.reshape(turn_count, per_turn, rows_here, kv_heads, head_dim)
    v_steps = v_piece.reshape(turn_count, per_turn, rows_here, kv_heads, head_dim)
    p_steps = k_pos.reshape(turn_count, per_turn, rows_here)

    def one_turn(carried, inputs_now):
        partial_value, row_top, row_total = source_partials(
            q_local, own_pos, inputs_now[0], inputs_now[1], inputs_now[2], head_dim
        )
        for member in range(per_turn):
            carried = absorb(carried, partial_value[member], row_top[member], row_total[member])
        return (carried, None)

    running, unused = lax.scan(one_turn, running, (k_steps, v_steps, p_steps))
    merged = running[2] / running[1][..., None]
    return merged.reshape(rows_here, kv_heads * common_values * head_dim).astype(jnp.bfloat16)


def solution(mesh):
    return jax.shard_map(
        shards,
        mesh=mesh,
        in_specs=(
            P(("groups", "ctx"), ("head", "rep")),
            P(("groups", "ctx"), ("head", "rep")),
            P(("groups", "ctx"), ("head", "rep")),
            P(),
        ),
        out_specs=P(("groups", "ctx"), ("head", "rep")),
        check_vma=False,
    )
```

profile of v0, /device:TPU:0, one launch (start us, length us, event | category | flops | bytes accessed | tf_op | source)
XLA Modules:
  0.0 60.6 jit_solution(10825627206917604020)
XLA Ops:
  0.0 0.0 copy-start
  0.0 0.8 %select_reduce_fusion.1 = s32[256]{0:T(256)S(1)} fusion(s32[8]{0:T(128)} %param.9, s32[256]{0:T(256)S(1)} %and_select_fusion.2), kind=kLoop, calls=%fused_computation.45 | loop fusion | flops 5888 | bytes 2080 | tf_op jit(solution)/shard_map/reduce_sum | solution.py:15
  0.8 1.2 %copy.30 = bf16[256,1024]{0,1:T(8,128)(2,1)S(1)} copy(bf16[256,1024]{1,0:T(8,128)(2,1)} %param.6) | data formatting | bytes 1048576 | tf_op args[0]
  2.1 1.0 %copy.32 = bf16[256,2,4,128]{3,0,2,1:T(8,128)(2,1)} copy(bf16[256,2,4,128]{0,3,2,1:T(8,128)(2,1)S(1)} %bitcast.99) | data formatting | bytes 1048576
  3.1 17.6 %all_gather.6 = bf16[1024,256]{1,0:T(8,128)(2,1)S(1)} all-gather(bf16[256,256]{1,0:T(8,128)(2,1)} %param.7), channel_id=1, replica_groups=mesh['groups'=2,'ctx'=4,'head'=2,'rep'=2] {'ctx'}, dimensions={0}, use_global_device_ids=true | all-gather | bytes 655360 | tf_op jit(solution)/shard_map/all_gather | solution.py:69
  20.7 0.9 %reshape.66 = bf16[2,2,256,2,128]{4,3,2,1,0:T(2,128)(2,1)} reshape(bf16[1024,256]{1,0:T(8,128)(2,1)S(1)} %all_gather.6) | data formatting | bytes 1048576 | tf_op jit(solution)/shard_map/reshape | solution.py:75
  21.6 16.6 %all_gather.7 = bf16[1024,256]{1,0:T(8,128)(2,1)S(1)} all-gather(bf16[256,256]{1,0:T(8,128)(2,1)} %param.8), channel_id=1, replica_groups=mesh['groups'=2,'ctx'=4,'head'=2,'rep'=2] {'ctx'}, dimensions={0}, use_global_device_ids=true | all-gather | bytes 655360 | tf_op jit(solution)/shard_map/all_gather | solution.py:70
  38.2 0.9 %reshape.68 = bf16[2,2,256,2,128]{4,3,2,1,0:T(2,128)(2,1)} reshape(bf16[1024,256]{1,0:T(8,128)(2,1)S(1)} %all_gather.7) | data formatting | bytes 1048576 | tf_op jit(solution)/shard_map/reshape | solution.py:76
  39.1 0.0 copy-done
  39.1 0.1 select_reduce_fusion
  39.3 20.2 %while.15 = (s32[]{:T(128)}, f32[256,2,4]{0,2,1:T(4,128)S(1)}, f32[256,2,4]{0,2,1:T(4,128)S(1)}, f32[256,2,4,128]{0,3,2,1:T(8,128)S(1)}, s32[2,2,256]{2,1,0:T(2,...) while((s32[]{:T(128)}, f32[256,2,4]{0,2,1:T(4,128)S(1)}, ...), condition=%wide.region_5.6_spmd.clone, body=%wide.region_2.5_spmd.clone.sunk | while | flops 549871616 | bytes 19995776 | solution.py:87
  39.3 1.4 %constant_dynamic-slice_fusion.3 = (bf16[1,2,256,2,128]{4,3,2,1,0:T(2,128)(2,1)S(1)}, bf16[1,2,256,2,128]{4,3,2,1,0:T(2,128)(2,1)S(1)}) fusion(bf16[2,2,256,2,128]{4,3,2,1,0:T(2,128)(2,1)} %get-tuple-element.251, s32[]{:T(128)} %get-tuple-element.232, bf16[2,2,256,2,128]{4,3,2,1,0:T(2,128)(2,1)} %get-tuple-element.249), kind=kLoop, calls=%fused_computation.38.clone.1 | loop fusion | bytes 1048580 | tf_op jit(solution)/shard_map/while/body/jit(dynamic_index_in_dim)/dynamic_slice | solution.py:87
  40.7 0.1 broadcast_compare_fusion.3
  40.8 1.9 %fusion.43 = (f32[2,256,2,4]{1,3,0,2:T(4,128)S(1)}, f32[2,2,256,256,4]{3,2,4,1,0:T(8,128)S(1)}) fusion(pred[2,256,256]{1,2,0:T(8,128)(4,1)S(1)} %broadcast_compare_fusion.3, bf16[256,2,4,128]{3,0,2,1:T(8,128)(2,1)} %get-tuple-element.250, bf16[1,2,256,2,128]{4,3,2,1,0:T(2,128)(2,1)S(1)} %get-tuple-element.209), kind=kOutput, calls=%fused_computation.2.clone.1 | convolution fusion | flops 271577088 | bytes 5128192 | tf_op jit(solution)/shard_map/while/body/eval_jaxpr/rhgd,cshd->crhgs/dot_general | solution.py:24
  42.7 1.2 %fusion.44 = (bf16[2,256,2,4,256]{1,4,3,0,2:T(8,128)(2,1)S(1)}, f32[2,256,2,4]{1,3,0,2:T(4,128)S(1)}) fusion(f32[2,2,256,256,4]{3,2,4,1,0:T(8,128)S(1)} %get-tuple-element.211, f32[2,256,2,4]{1,3,0,2:T(4,128)S(1)} %get-tuple-element.210, pred[2,256,256]{1,2,0:T(8,128)(4,1)S(1)} %broadcast_compare_fusion.3), kind=kLoop, calls=%fused_computation.3.clone.1 | loop fusion | flops 6287360 | bytes 6455296 | tf_op jit(solution)/shard_map/while/body/eval_jaxpr/convert_element_type | solution.py:34
  43.9 0.9 %copy.63 = bf16[1,2,256,2,128]{2,4,3,1,0:T(8,128)(2,1)} copy(bf16[1,2,256,2,128]{4,3,2,1,0:T(2,128)(2,1)S(1)} %get-tuple-element.216) | data formatting | bytes 524288 | tf_op jit(solution)/shard_map/while/body/jit(dynamic_index_in_dim)/dynamic_slice | solution.py:87
  44.8 2.4 %fusion.46 = bf16[2,256,2,4,128]{1,4,3,2,0:T(8,128)(2,1)} fusion(bf16[2,256,2,4,256]{1,4,3,0,2:T(8,128)(2,1)S(1)} %get-tuple-element.215, bf16[1,2,256,2,128]{2,4,3,1,0:T(8,128)(2,1)} %copy.63, f32[2,256,2,4]{1,3,0,2:T(4,128)S(1)} %get-tuple-element.212), kind=kOutput, calls=%fused_computation.6.clone.1 | convolution fusion | flops 269488128 | bytes 3424256 | tf_op jit(solution)/shard_map/while/body/eval_jaxpr/crhgs,cshd->crhgd/dot_general | solution.py:32
  47.2 2.1 %fusion.47 = f32[256,2,4,128]{0,3,2,1:T(8,128)S(1)} fusion(f32[256,2,4,128]{0,3,2,1:T(8,128)S(1)} %get-tuple-element.235, bf16[2,256,2,4,128]{1,4,3,2,0:T(8,128)(2,1)} %fusion.46, f32[256,2,4]{0,2,1:T(4,128)S(1)} %get-tuple-element.217, f32[256,2,4]{0,2,1:T(4,128)S(1)} %get-tuple-element.218, f32[256,2,4]{0,2,1:T(4,128)S(1)} %get-tuple-element.219, ...), kind=kLoop, calls=%fused_computation.10.clone.1 | loop fusion | flops 2359296 | bytes 3178497 | tf_op jit(solution)/shard_map/while/body/eval_jaxpr/add | solution.py:50
  49.4 1.4 %constant_dynamic-slice_fusion.3 = (bf16[1,2,256,2,128]{4,3,2,1,0:T(2,128)(2,1)S(1)}, bf16[1,2,256,2,128]{4,3,2,1,0:T(2,128)(2,1)S(1)}) fusion(bf16[2,2,256,2,128]{4,3,2,1,0:T(2,128)(2,1)} %get-tuple-element.251, s32[]{:T(128)} %get-tuple-element.232, bf16[2,2,256,2,128]{4,3,2,1,0:T(2,128)(2,1)} %get-tuple-element.249), kind=kLoop, calls=%fused_computation.38.clone.1 | loop fusion | bytes 1048580 | tf_op jit(solution)/shard_map/while/body/jit(dynamic_index_in_dim)/dynamic_slice | solution.py:87
  50.8 0.1 broadcast_compare_fusion.3
  50.9 1.9 %fusion.43 = (f32[2,256,2,4]{1,3,0,2:T(4,128)S(1)}, f32[2,2,256,256,4]{3,2,4,1,0:T(8,128)S(1)}) fusion(pred[2,256,256]{1,2,0:T(8,128)(4,1)S(1)} %broadcast_compare_fusion.3, bf16[256,2,4,128]{3,0,2,1:T(8,128)(2,1)} %get-tuple-element.250, bf16[1,2,256,2,128]{4,3,2,1,0:T(2,128)(2,1)S(1)} %get-tuple-element.209), kind=kOutput, calls=%fused_computation.2.clone.1 | convolution fusion | flops 271577088 | bytes 5128192 | tf_op jit(solution)/shard_map/while/body/eval_jaxpr/rhgd,cshd->crhgs/dot_general | solution.py:24
  52.8 1.2 %fusion.44 = (bf16[2,256,2,4,256]{1,4,3,0,2:T(8,128)(2,1)S(1)}, f32[2,256,2,4]{1,3,0,2:T(4,128)S(1)}) fusion(f32[2,2,256,256,4]{3,2,4,1,0:T(8,128)S(1)} %get-tuple-element.211, f32[2,256,2,4]{1,3,0,2:T(4,128)S(1)} %get-tuple-element.210, pred[2,256,256]{1,2,0:T(8,128)(4,1)S(1)} %broadcast_compare_fusion.3), kind=kLoop, calls=%fused_computation.3.clone.1 | loop fusion | flops 6287360 | bytes 6455296 | tf_op jit(solution)/shard_map/while/body/eval_jaxpr/convert_element_type | solution.py:34
  54.0 0.9 %copy.63 = bf16[1,2,256,2,128]{2,4,3,1,0:T(8,128)(2,1)} copy(bf16[1,2,256,2,128]{4,3,2,1,0:T(2,128)(2,1)S(1)} %get-tuple-element.216) | data formatting | bytes 524288 | tf_op jit(solution)/shard_map/while/body/jit(dynamic_index_in_dim)/dynamic_slice | solution.py:87
  54.9 2.4 %fusion.46 = bf16[2,256,2,4,128]{1,4,3,2,0:T(8,128)(2,1)} fusion(bf16[2,256,2,4,256]{1,4,3,0,2:T(8,128)(2,1)S(1)} %get-tuple-element.215, bf16[1,2,256,2,128]{2,4,3,1,0:T(8,128)(2,1)} %copy.63, f32[2,256,2,4]{1,3,0,2:T(4,128)S(1)} %get-tuple-element.212), kind=kOutput, calls=%fused_computation.6.clone.1 | convolution fusion | flops 269488128 | bytes 3424256 | tf_op jit(solution)/shard_map/while/body/eval_jaxpr/crhgs,cshd->crhgd/dot_general | solution.py:32
  57.3 2.1 %fusion.47 = f32[256,2,4,128]{0,3,2,1:T(8,128)S(1)} fusion(f32[256,2,4,128]{0,3,2,1:T(8,128)S(1)} %get-tuple-element.235, bf16[2,256,2,4,128]{1,4,3,2,0:T(8,128)(2,1)} %fusion.46, f32[256,2,4]{0,2,1:T(4,128)S(1)} %get-tuple-element.217, f32[256,2,4]{0,2,1:T(4,128)S(1)} %get-tuple-element.218, f32[256,2,4]{0,2,1:T(4,128)S(1)} %get-tuple-element.219, ...), kind=kLoop, calls=%fused_computation.10.clone.1 | loop fusion | flops 2359296 | bytes 3178497 | tf_op jit(solution)/shard_map/while/body/eval_jaxpr/add | solution.py:50
  59.5 0.1 divide_convert_fusion
  59.6 1.0 %copy.39 = bf16[256,1024]{1,0:T(8,128)(2,1)} copy(bf16[256,1024]{0,1:T(8,128)(2,1)S(1)} %bitcast.98) | data formatting | bytes 1048576 | tf_op jit(solution)/shard_map/convert_element_type | solution.py:89
  (13 shorter events, 0.1 us)
Async XLA Ops:
  0.0 39.1 %copy-start = (s32[8]{0:T(128)S(1)}, s32[8]{0:T(128)}, u32[]{:S(2)}) copy-start(s32[8]{0:T(128)} %param.9) | copy-start | bytes 100
where the time goes:
time: 61 us; the launch traced here: 60.6 us
  blocking collectives  34.1 us (56%)
  local copies, waits for them, and re-layouts  9.69 us (16%)
  matrix products  8.65 us (14%)
  other arithmetic  7.94 us (13%)
    all_gather x1, blocking collectives, shards(): k_piece = lax.all_gather(keys, 'ctx', axis=0, tiled=True)  17.6 us
    all_gather x1, blocking collectives, shards(): v_piece = lax.all_gather(values, 'ctx', axis=0, tiled=True)  16.6 us
    dot_general x2, matrix products, source_partials(): jnp.einsum('crhgs,cshd->crhgd', weights.astype(jnp.bfloat16), value_group...  4.85 us
    dynamic_slice x4, local copies, waits for them, and re-layouts, shards(): running, unused = lax.scan(one_turn, running, (k_steps, v_steps, p_steps))  4.53 us
    add x2, other arithmetic, absorb(): run_sum * rescale[..., None]  4.23 us
    dot_general x2, matrix products, source_partials(): jnp.einsum('rhgd,cshd->crhgs', query_block, key_group, preferred_element_...  3.8 us
    convert_element_type x2, other arithmetic, source_partials(): weights.astype(jnp.bfloat16)  2.34 us
    unnamed x4, local copies, waits for them, and re-layouts  2.27 us

commit v1 on v0

--- a/solution.py
+++ b/solution.py
@@ -66,8 +66,11 @@
         jnp.zeros((rows_here, kv_heads, common_values, head_dim), jnp.float32),
     )
     running = initial
-    k_piece = lax.all_gather(keys, "ctx", axis=0, tiled=True)
-    v_piece = lax.all_gather(values, "ctx", axis=0, tiled=True)
+    k_piece, v_piece = jnp.split(
+        lax.all_gather(jnp.concatenate([keys, values], axis=1), "ctx", axis=0, tiled=True),
+        [keys.shape[1]],
+        axis=1,
+    )
     shard_count = k_piece.shape[0] // rows_here
     per_turn = 2
     turn_count = shard_count // per_turn

time: 61 us -> 71.3 us (1.17)
  blocking collectives: 34.1 us -> 0 us
  waiting for transfers between devices: 0 us -> 27.5 us
  between operations: 0.06 us -> 13.5 us
  other arithmetic: 7.94 us -> 10.2 us
  local copies, waits for them, and re-layouts: 9.69 us -> 10.9 us
    all_gather x2 -> x0, blocking collectives: 34.1 us -> none  [the longest x1 17.6 us: shards(): k_piece = lax.all_gather(keys, 'ctx', axis=0, tiled=True)]
    all_gather x0 -> x1, waiting for transfers between devices: none -> 27.5 us  [shards(): lax.all_gather(jnp.concatenate([keys, values], axis=1), 'ctx', axis=0, ti...]
    concatenate x0 -> x1, other arithmetic: none -> 1.69 us  [shards(): jnp.concatenate([keys, values], axis=1)]
    split x0 -> x1, local copies, waits for them, and re-layouts: none -> 1.27 us  [shards(): jnp.split(lax.all_gather(jnp.concatenate([keys, values], axis=1), 'ctx',...]
    unnamed x4 -> x2, local copies, waits for them, and re-layouts: 2.27 us -> 2.27 us
  transfers between devices with their start and end apart: 0 -> 1, of which waited for: 0 -> 1; matrix products, arithmetic and copies ran while one was open for 0% -> 5% of each run, Pallas kernels for 0% -> 0%
where the time goes in v1:
time: 71.3 us; the launch traced here: 70.9 us
  waiting for transfers between devices  27.5 us (39%)
  between operations  13.5 us (19%)
  local copies, waits for them, and re-layouts  10.9 us (15%)
  other arithmetic  10.2 us (14%)
  matrix products  8.61 us (12%)
    all_gather x1, waiting for transfers between devices, shards(): lax.all_gather(jnp.concatenate([keys, values], axis=1), 'ctx', axis=0, ti...  27.5 us
    dot_general x2, matrix products, source_partials(): jnp.einsum('crhgs,cshd->crhgd', weights.astype(jnp.bfloat16), value_group...  4.85 us
    dynamic_slice x4, local copies, waits for them, and re-layouts, shards(): running, unused = lax.scan(one_turn, running, (k_steps, v_steps, p_steps))  4.53 us
    add x2, other arithmetic, absorb(): run_sum * rescale[..., None]  4.23 us
    dot_general x2, matrix products, source_partials(): jnp.einsum('rhgd,cshd->crhgs', query_block, key_group, preferred_element_...  3.77 us
    convert_element_type x2, other arithmetic, source_partials(): weights.astype(jnp.bfloat16)  2.34 us
    unnamed x2, local copies, waits for them, and re-layouts  2.27 us
    concatenate x1, other arithmetic, shards(): jnp.concatenate([keys, values], axis=1)  1.69 us
  transfers between devices with their start and end apart: 1, of which 1 were waited for; matrix products, arithmetic and copies ran while one was open for 5% of the time, Pallas kernels for 0%

profile of v1, /device:TPU:0, one launch (start us, length us, event | category | flops | bytes accessed | tf_op | source)
XLA Modules:
  0.0 70.9 jit_solution(11305848871449782462)
XLA Ops:
  6.5 0.0 all-gather.2.cloned.1.call-start
  6.5 1.7 %pad_maximum_fusion = bf16[256,512]{1,0:T(8,128)(2,1)} fusion(bf16[256,256]{1,0:T(8,128)(2,1)} %param.8, bf16[256,256]{1,0:T(8,128)(2,1)} %param.7), kind=kLoop, calls=%fused_computation.41 | loop fusion | flops 524288 | bytes 524288 | tf_op jit(solution)/shard_map/concatenate | solution.py:70
  8.2 0.0 all-gather.2.cloned.1.call-update
  8.3 1.2 %copy.30 = bf16[256,1024]{0,1:T(8,128)(2,1)S(1)} copy(bf16[256,1024]{1,0:T(8,128)(2,1)} %param.6) | data formatting | bytes 1048576 | tf_op args[0]
  9.5 1.0 %copy.32 = bf16[256,2,4,128]{3,0,2,1:T(8,128)(2,1)} copy(bf16[256,2,4,128]{0,3,2,1:T(8,128)(2,1)S(1)} %bitcast.99) | data formatting | bytes 1048576
  10.6 0.7 %select_reduce_fusion = s32[1024]{0:T(1024)S(1)} fusion(s32[8]{0:T(128)} %param.9, s32[1024]{0:T(1024)S(1)} %add_select_fusion), kind=kLoop, calls=%fused_computation.42 | loop fusion | flops 23552 | bytes 8224 | tf_op jit(solution)/shard_map/reduce_sum | solution.py:15
  11.3 0.7 %select_reduce_fusion.1 = s32[256]{0:T(256)S(1)} fusion(s32[8]{0:T(128)} %param.9, s32[256]{0:T(256)S(1)} %and_select_fusion.2), kind=kLoop, calls=%fused_computation.46 | loop fusion | flops 5888 | bytes 2080 | tf_op jit(solution)/shard_map/reduce_sum | solution.py:15
  12.1 27.5 %all-gather.2.cloned.1.call-done = bf16[1024,512]{1,0:T(8,128)(2,1)} async-done(((bf16[256,512]{1,0:T(8,128)(2,1)}), bf16[1024,512]{1,0:T(8,128)(2,1)}) %all-gather.2.cloned.1.call-update) | async-done | bytes 1048592 | tf_op jit(solution)/shard_map/all_gather | solution.py:70
  39.6 1.3 %fusion.31 = (bf16[1024,256]{1,0:T(8,128)(2,1)S(1)}, bf16[1024,256]{1,0:T(8,128)(2,1)S(1)}) fusion(bf16[1024,512]{1,0:T(8,128)(2,1)} %all-gather.2.cloned.1.call-done), kind=kLoop, calls=%fused_computation.68 | loop fusion | bytes 2097152 | tf_op jit(solution)/shard_map/split | solution.py:69
  40.9 0.9 %reshape.66 = bf16[2,2,256,2,128]{4,3,2,1,0:T(2,128)(2,1)} reshape(bf16[1024,256]{1,0:T(8,128)(2,1)S(1)} %get-tuple-element.143) | data formatting | bytes 1048576 | tf_op jit(solution)/shard_map/reshape | solution.py:78
  41.8 0.9 %reshape.68 = bf16[2,2,256,2,128]{4,3,2,1,0:T(2,128)(2,1)} reshape(bf16[1024,256]{1,0:T(8,128)(2,1)S(1)} %get-tuple-element.142) | data formatting | bytes 1048576 | tf_op jit(solution)/shard_map/reshape | solution.py:79
  42.8 20.1 %while.15 = (s32[]{:T(128)}, f32[256,2,4]{0,2,1:T(4,128)S(1)}, f32[256,2,4]{0,2,1:T(4,128)S(1)}, f32[256,2,4,128]{0,3,2,1:T(8,128)S(1)}, s32[2,2,256]{2,1,0:T(2,...) while((s32[]{:T(128)}, f32[256,2,4]{0,2,1:T(4,128)S(1)}, ...), condition=%wide.region_5.6_spmd.clone, body=%wide.region_2.5_spmd.clone.sunk | while | flops 549871616 | bytes 19995776 | solution.py:90
  42.8 1.4 %constant_dynamic-slice_fusion.3 = (bf16[1,2,256,2,128]{4,3,2,1,0:T(2,128)(2,1)S(1)}, bf16[1,2,256,2,128]{4,3,2,1,0:T(2,128)(2,1)S(1)}) fusion(bf16[2,2,256,2,128]{4,3,2,1,0:T(2,128)(2,1)} %get-tuple-element.253, s32[]{:T(128)} %get-tuple-element.234, bf16[2,2,256,2,128]{4,3,2,1,0:T(2,128)(2,1)} %get-tuple-element.251), kind=kLoop, calls=%fused_computation.38.clone.1 | loop fusion | bytes 1048580 | tf_op jit(solution)/shard_map/while/body/jit(dynamic_index_in_dim)/dynamic_slice | solution.py:90
  44.2 0.1 broadcast_compare_fusion.3
  44.3 1.9 %fusion.44 = (f32[2,256,2,4]{1,3,0,2:T(4,128)S(1)}, f32[2,2,256,256,4]{3,2,4,1,0:T(8,128)S(1)}) fusion(pred[2,256,256]{1,2,0:T(8,128)(4,1)S(1)} %broadcast_compare_fusion.3, bf16[256,2,4,128]{3,0,2,1:T(8,128)(2,1)} %get-tuple-element.252, bf16[1,2,256,2,128]{4,3,2,1,0:T(2,128)(2,1)S(1)} %get-tuple-element.211), kind=kOutput, calls=%fused_computation.2.clone.1 | convolution fusion | flops 271577088 | bytes 5128192 | tf_op jit(solution)/shard_map/while/body/eval_jaxpr/rhgd,cshd->crhgs/dot_general | solution.py:24
  46.2 1.2 %fusion.45 = (bf16[2,256,2,4,256]{1,4,3,0,2:T(8,128)(2,1)S(1)}, f32[2,256,2,4]{1,3,0,2:T(4,128)S(1)}) fusion(f32[2,2,256,256,4]{3,2,4,1,0:T(8,128)S(1)} %get-tuple-element.213, f32[2,256,2,4]{1,3,0,2:T(4,128)S(1)} %get-tuple-element.212, pred[2,256,256]{1,2,0:T(8,128)(4,1)S(1)} %broadcast_compare_fusion.3), kind=kLoop, calls=%fused_computation.3.clone.1 | loop fusion | flops 6287360 | bytes 6455296 | tf_op jit(solution)/shard_map/while/body/eval_jaxpr/convert_element_type | solution.py:34
  47.4 0.9 %copy.63 = bf16[1,2,256,2,128]{2,4,3,1,0:T(8,128)(2,1)} copy(bf16[1,2,256,2,128]{4,3,2,1,0:T(2,128)(2,1)S(1)} %get-tuple-element.218) | data formatting | bytes 524288 | tf_op jit(solution)/shard_map/while/body/jit(dynamic_index_in_dim)/dynamic_slice | solution.py:90
  48.3 2.4 %fusion.47 = bf16[2,256,2,4,128]{1,4,3,2,0:T(8,128)(2,1)} fusion(bf16[2,256,2,4,256]{1,4,3,0,2:T(8,128)(2,1)S(1)} %get-tuple-element.217, bf16[1,2,256,2,128]{2,4,3,1,0:T(8,128)(2,1)} %copy.63, f32[2,256,2,4]{1,3,0,2:T(4,128)S(1)} %get-tuple-element.214), kind=kOutput, calls=%fused_computation.6.clone.1 | convolution fusion | flops 269488128 | bytes 3424256 | tf_op jit(solution)/shard_map/while/body/eval_jaxpr/crhgs,cshd->crhgd/dot_general | solution.py:32
  50.7 2.1 %fusion.48 = f32[256,2,4,128]{0,3,2,1:T(8,128)S(1)} fusion(f32[256,2,4,128]{0,3,2,1:T(8,128)S(1)} %get-tuple-element.237, bf16[2,256,2,4,128]{1,4,3,2,0:T(8,128)(2,1)} %fusion.47, f32[256,2,4]{0,2,1:T(4,128)S(1)} %get-tuple-element.219, f32[256,2,4]{0,2,1:T(4,128)S(1)} %get-tuple-element.220, f32[256,2,4]{0,2,1:T(4,128)S(1)} %get-tuple-element.221, ...), kind=kLoop, calls=%fused_computation.10.clone.1 | loop fusion | flops 2359296 | bytes 3178497 | tf_op jit(solution)/shard_map/while/body/eval_jaxpr/add | solution.py:50
  52.8 1.4 %constant_dynamic-slice_fusion.3 = (bf16[1,2,256,2,128]{4,3,2,1,0:T(2,128)(2,1)S(1)}, bf16[1,2,256,2,128]{4,3,2,1,0:T(2,128)(2,1)S(1)}) fusion(bf16[2,2,256,2,128]{4,3,2,1,0:T(2,128)(2,1)} %get-tuple-element.253, s32[]{:T(128)} %get-tuple-element.234, bf16[2,2,256,2,128]{4,3,2,1,0:T(2,128)(2,1)} %get-tuple-element.251), kind=kLoop, calls=%fused_computation.38.clone.1 | loop fusion | bytes 1048580 | tf_op jit(solution)/shard_map/while/body/jit(dynamic_index_in_dim)/dynamic_slice | solution.py:90
  54.3 0.1 broadcast_compare_fusion.3
  54.4 1.9 %fusion.44 = (f32[2,256,2,4]{1,3,0,2:T(4,128)S(1)}, f32[2,2,256,256,4]{3,2,4,1,0:T(8,128)S(1)}) fusion(pred[2,256,256]{1,2,0:T(8,128)(4,1)S(1)} %broadcast_compare_fusion.3, bf16[256,2,4,128]{3,0,2,1:T(8,128)(2,1)} %get-tuple-element.252, bf16[1,2,256,2,128]{4,3,2,1,0:T(2,128)(2,1)S(1)} %get-tuple-element.211), kind=kOutput, calls=%fused_computation.2.clone.1 | convolution fusion | flops 271577088 | bytes 5128192 | tf_op jit(solution)/shard_map/while/body/eval_jaxpr/rhgd,cshd->crhgs/dot_general | solution.py:24
  56.3 1.2 %fusion.45 = (bf16[2,256,2,4,256]{1,4,3,0,2:T(8,128)(2,1)S(1)}, f32[2,256,2,4]{1,3,0,2:T(4,128)S(1)}) fusion(f32[2,2,256,256,4]{3,2,4,1,0:T(8,128)S(1)} %get-tuple-element.213, f32[2,256,2,4]{1,3,0,2:T(4,128)S(1)} %get-tuple-element.212, pred[2,256,256]{1,2,0:T(8,128)(4,1)S(1)} %broadcast_compare_fusion.3), kind=kLoop, calls=%fused_computation.3.clone.1 | loop fusion | flops 6287360 | bytes 6455296 | tf_op jit(solution)/shard_map/while/body/eval_jaxpr/convert_element_type | solution.py:34
  57.5 0.9 %copy.63 = bf16[1,2,256,2,128]{2,4,3,1,0:T(8,128)(2,1)} copy(bf16[1,2,256,2,128]{4,3,2,1,0:T(2,128)(2,1)S(1)} %get-tuple-element.218) | data formatting | bytes 524288 | tf_op jit(solution)/shard_map/while/body/jit(dynamic_index_in_dim)/dynamic_slice | solution.py:90
  58.3 2.4 %fusion.47 = bf16[2,256,2,4,128]{1,4,3,2,0:T(8,128)(2,1)} fusion(bf16[2,256,2,4,256]{1,4,3,0,2:T(8,128)(2,1)S(1)} %get-tuple-element.217, bf16[1,2,256,2,128]{2,4,3,1,0:T(8,128)(2,1)} %copy.63, f32[2,256,2,4]{1,3,0,2:T(4,128)S(1)} %get-tuple-element.214), kind=kOutput, calls=%fused_computation.6.clone.1 | convolution fusion | flops 269488128 | bytes 3424256 | tf_op jit(solution)/shard_map/while/body/eval_jaxpr/crhgs,cshd->crhgd/dot_general | solution.py:32
  60.8 2.1 %fusion.48 = f32[256,2,4,128]{0,3,2,1:T(8,128)S(1)} fusion(f32[256,2,4,128]{0,3,2,1:T(8,128)S(1)} %get-tuple-element.237, bf16[2,256,2,4,128]{1,4,3,2,0:T(8,128)(2,1)} %fusion.47, f32[256,2,4]{0,2,1:T(4,128)S(1)} %get-tuple-element.219, f32[256,2,4]{0,2,1:T(4,128)S(1)} %get-tuple-element.220, f32[256,2,4]{0,2,1:T(4,128)S(1)} %get-tuple-element.221, ...), kind=kLoop, calls=%fused_computation.10.clone.1 | loop fusion | flops 2359296 | bytes 3178497 | tf_op jit(solution)/shard_map/while/body/eval_jaxpr/add | solution.py:50
  62.9 0.1 divide_convert_fusion
  63.0 1.0 %copy.39 = bf16[256,1024]{1,0:T(8,128)(2,1)} copy(bf16[256,1024]{0,1:T(8,128)(2,1)S(1)} %bitcast.98) | data formatting | bytes 1048576 | tf_op jit(solution)/shard_map/convert_element_type | solution.py:92
  (13 shorter events, 0.1 us)
Async XLA Ops:
  6.5 33.1 %all-gather.2.cloned.1.call-start = ((), (), s32[]{:S(2)}) async-start(), calls=%async_computation | async-start | bytes 1310720 | tf_op jit(solution)/shard_map/all_gather | solution.py:70
Sparse Core Ops, SparseCore 0:
  8.9 30.6 all-gather.1
